TPU v7x, 256 devices: a whole 4x4x8 slice. The times are simulated.
256 devices in a mesh: grp: 4 (over y), dev: 64 (over x, z, core).
Axes of the slice: x: 4, y: 4, z: 8, core: 2. Of those that a mesh axis runs over, the one named last changes fastest.
Arguments:
- labels: int32 [256, 65536], P(('grp', 'dev')), may hold values from 0 to 16383, as said below
- present: int32 [256, 512], P(('grp', 'dev')), may hold values from 0 to 16383, as said below
- values: bfloat16 [256, 64, 65536], P(('grp', 'dev')), may hold values from -8 to 8
Outputs:
- zone_mean: float32 [64, 16384], P(None, 'dev')
Inputs may be any that keep to these rules, and one draw needn't show every extreme that they name: `present`: each tile's 512 listed zones are distinct and ascending; at most 16 of them lie in one block of 256 consecutive zones, and in each group of 64 consecutive tiles one such block holds exactly 16 zones of every tile of the group. `labels`: every label of a tile is one of that tile's listed zones.
All inputs are finite; a program needn't handle non-finite values.
Results may differ from a plain program's by a relative error of at most 0.0003.
Values sent between devices are 32-bit elements; how exact they have to be, the bound alone decides.
A program may use at most 64 MiB of HBM per device.

v0:
```python
import math

import jax
import jax.numpy as jnp
from jax import lax
from jax.sharding import PartitionSpec as P

ZONES = 16384


def sent_together(arrays, axis, split_dim, concat_dim, along):
    widths = [math.prod(a.shape[along:]) for a in arrays]
    both = jnp.concatenate(
        [a.reshape(*a.shape[:along], w) for a, w in zip(arrays, widths)], axis=along
    )
    whole = lax.all_to_all(both, axis, split_axis=split_dim, concat_axis=concat_dim, tiled=True)
    parts = jnp.split(whole, [sum(widths[:k]) for k in range(1, len(widths))], axis=along)
    return tuple((b.reshape(*whole.shape[:along], *a.shape[along:]) for a, b in zip(arrays, parts)))


def copy_for_each(array, axis):
    copies = jnp.broadcast_to(array, (lax.axis_size(axis), *array.shape))
    return lax.all_to_all(copies, axis, split_axis=0, concat_axis=0, tiled=True)


def taken_together(array, axis):
    return copy_for_each(array, axis).sum(axis=0)


def together(arrays, axis):
    flat, at, finished = (jnp.concatenate([a.reshape(-1) for a in arrays]), 0, [])
    so_far = taken_together(flat, axis)
    for a in arrays:
        finished.append(so_far[at : at + a.size].reshape(a.shape))
        at += a.size
    return tuple(finished)


def body(labels, present, values):
    label_row = labels[0]
    present_ids = present[0]
    pixel_values = values[0]
    time_steps, pixel_count = pixel_values.shape
    slot_count = present_ids.shape[0]
    owner_count = lax.axis_size("dev")
    range_width = ZONES // owner_count
    block_size = min(pixel_count, 8192)

    def accumulate(block_index, carry):
        partial_sums, partial_counts = carry
        block_labels = lax.dynamic_slice_in_dim(label_row, block_index * block_size, block_size)
        block_values = lax.dynamic_slice_in_dim(
            pixel_values, block_index * block_size, block_size, 1
        )
        one_hot = (present_ids[:, None] == block_labels[None, :]).astype(jnp.bfloat16)
        partial_sums = partial_sums + lax.dot_general(
            block_values, one_hot, (((1,), (1,)), ((), ())), preferred_element_type=jnp.float32
        )
        partial_counts = partial_counts + jnp.sum(one_hot, axis=1, dtype=jnp.float32)
        return (partial_sums, partial_counts)

    start = (
        jnp.zeros((time_steps, slot_count), jnp.float32),
        jnp.zeros((slot_count,), jnp.float32),
    )
    partial_sums, partial_counts = lax.fori_loop(0, pixel_count // block_size, accumulate, start)
    owner_of = present_ids // range_width
    local_place = present_ids % range_width
    capacity = 2 * slot_count // owner_count
    owner_ids = jnp.arange(owner_count, dtype=jnp.int32)
    first_slot = jnp.sum((owner_of[:, None] < owner_ids[None, :]).astype(jnp.int32), axis=0)
    per_owner = jnp.sum((owner_of[:, None] == owner_ids[None, :]).astype(jnp.int32), axis=0)
    slot_ids = jnp.arange(capacity, dtype=jnp.int32)
    usable = slot_ids[None, :] < per_owner[:, None]
    source_slot = jnp.clip(first_slot[:, None] + slot_ids[None, :], 0, slot_count - 1).reshape(-1)
    picked = jnp.take(partial_sums, source_slot, axis=1).reshape(time_steps, owner_count, capacity)
    send_sums = jnp.where(usable[None], picked, 0.0).transpose(1, 0, 2)
    send_counts = jnp.where(
        usable, jnp.take(partial_counts, source_slot).reshape(owner_count, capacity), 0.0
    )
    send_place = jnp.where(
        usable,
        jnp.take(local_place, source_slot).reshape(owner_count, capacity).astype(jnp.float32),
        -1.0,
    )
    got_sums, got_counts, got_place = sent_together(
        (send_sums, send_counts, send_place), "dev", 0, 0, 1
    )
    placing = (
        got_place.reshape(-1)[:, None] == jnp.arange(range_width, dtype=jnp.float32)[None, :]
    ).astype(jnp.float32)
    flat_sums = got_sums.transpose(1, 0, 2).reshape(time_steps, owner_count * capacity)
    owner_sums = jnp.dot(flat_sums, placing, precision=lax.Precision.HIGHEST)
    owner_counts = jnp.dot(got_counts.reshape(-1), placing, precision=lax.Precision.HIGHEST)
    total_sums, total_counts = together((owner_sums, owner_counts), "grp")
    return total_sums / jnp.maximum(total_counts, 1.0)[None, :]


def solution(mesh):
    return jax.shard_map(
        body,
        mesh=mesh,
        in_specs=(P(("grp", "dev"), None), P(("grp", "dev"), None), P(("grp", "dev"), None, None)),
        out_specs=P(None, "dev"),
        check_vma=False,
    )
```

profile of v0, /device:TPU:1, one launch (start us, length us, event | category | flops | bytes accessed | tf_op | source)
XLA Modules:
  0.0 117.7 jit_solution(11151579771615321174)
XLA Ops:
  1.1 60.3 %while.16 = (s32[]{:T(128)}, f32[64,512]{1,0:T(8,128)S(1)}, f32[512]{0:T(512)S(1)}, bf16[64,65536]{1,0:T(8,128)(2,1)}, s32[1,512]{1,0:T(1,128)}, /*index=5*/s32[...) while((s32[]{:T(128)}, f32[64,512]{1,0:T(8,128)S(1)}, f32[512]{0:T(512)S(1)}, ...), condition=%wide.region_4.5_spmd.clone, body=%wide.region_2.4_spmd.clone.sunk | while | flops 557908480 | bytes 1454246 | solution.py:66
  1.1 0.8 dynamic_slice.21
  1.8 4.3 %fusion.21 = f32[64,512]{1,0:T(8,128)S(1)} fusion(s32[8192]{0:T(1024)S(1)} %dynamic_slice.21, s32[512]{0:T(512)} %bitcast.36, bf16[64,65536]{1,0:T(8,128)(2,1)} %get-tuple-element.220, s32[]{:T(128)S(6)} %select_n.101, f32[64,512]{1,0:T(8,128)S(1)} %get-tuple-element.208, pred[]{:T(512)S(6)} %compare.11), kind=kOutput, calls=%fused_computation.9.clone.1 | convolution fusion | flops 541130752 | bytes 1345541 | tf_op jit(solution)/shard_map/while/body/eval_jaxpr/dot_general | solution.py:56
  6.1 2.5 %convert_reduce_fusion.4 = f32[512]{0:T(512)S(1)} fusion(s32[8192]{0:T(1024)S(1)} %dynamic_slice.21, s32[512]{0:T(512)} %bitcast.37), kind=kLoop, calls=%fused_computation.6.clone.1 | loop fusion | flops 16776704 | bytes 36864 | tf_op jit(solution)/shard_map/while/body/eval_jaxpr/reduce_sum | solution.py:59
  9.4 4.3 %fusion.21 = f32[64,512]{1,0:T(8,128)S(1)} fusion(s32[8192]{0:T(1024)S(1)} %dynamic_slice.21, s32[512]{0:T(512)} %bitcast.36, bf16[64,65536]{1,0:T(8,128)(2,1)} %get-tuple-element.220, s32[]{:T(128)S(6)} %select_n.101, f32[64,512]{1,0:T(8,128)S(1)} %get-tuple-element.208, pred[]{:T(512)S(6)} %compare.11), kind=kOutput, calls=%fused_computation.9.clone.1 | convolution fusion | flops 541130752 | bytes 1345541 | tf_op jit(solution)/shard_map/while/body/eval_jaxpr/dot_general | solution.py:56
  13.6 2.5 %convert_reduce_fusion.4 = f32[512]{0:T(512)S(1)} fusion(s32[8192]{0:T(1024)S(1)} %dynamic_slice.21, s32[512]{0:T(512)} %bitcast.37), kind=kLoop, calls=%fused_computation.6.clone.1 | loop fusion | flops 16776704 | bytes 36864 | tf_op jit(solution)/shard_map/while/body/eval_jaxpr/reduce_sum | solution.py:59
  16.9 4.3 %fusion.21 = f32[64,512]{1,0:T(8,128)S(1)} fusion(s32[8192]{0:T(1024)S(1)} %dynamic_slice.21, s32[512]{0:T(512)} %bitcast.36, bf16[64,65536]{1,0:T(8,128)(2,1)} %get-tuple-element.220, s32[]{:T(128)S(6)} %select_n.101, f32[64,512]{1,0:T(8,128)S(1)} %get-tuple-element.208, pred[]{:T(512)S(6)} %compare.11), kind=kOutput, calls=%fused_computation.9.clone.1 | convolution fusion | flops 541130752 | bytes 1345541 | tf_op jit(solution)/shard_map/while/body/eval_jaxpr/dot_general | solution.py:56
  21.2 2.5 %convert_reduce_fusion.4 = f32[512]{0:T(512)S(1)} fusion(s32[8192]{0:T(1024)S(1)} %dynamic_slice.21, s32[512]{0:T(512)} %bitcast.37), kind=kLoop, calls=%fused_computation.6.clone.1 | loop fusion | flops 16776704 | bytes 36864 | tf_op jit(solution)/shard_map/while/body/eval_jaxpr/reduce_sum | solution.py:59
  24.5 4.3 %fusion.21 = f32[64,512]{1,0:T(8,128)S(1)} fusion(s32[8192]{0:T(1024)S(1)} %dynamic_slice.21, s32[512]{0:T(512)} %bitcast.36, bf16[64,65536]{1,0:T(8,128)(2,1)} %get-tuple-element.220, s32[]{:T(128)S(6)} %select_n.101, f32[64,512]{1,0:T(8,128)S(1)} %get-tuple-element.208, pred[]{:T(512)S(6)} %compare.11), kind=kOutput, calls=%fused_computation.9.clone.1 | convolution fusion | flops 541130752 | bytes 1345541 | tf_op jit(solution)/shard_map/while/body/eval_jaxpr/dot_general | solution.py:56
  28.7 2.5 %convert_reduce_fusion.4 = f32[512]{0:T(512)S(1)} fusion(s32[8192]{0:T(1024)S(1)} %dynamic_slice.21, s32[512]{0:T(512)} %bitcast.37), kind=kLoop, calls=%fused_computation.6.clone.1 | loop fusion | flops 16776704 | bytes 36864 | tf_op jit(solution)/shard_map/while/body/eval_jaxpr/reduce_sum | solution.py:59
  32.0 4.3 %fusion.21 = f32[64,512]{1,0:T(8,128)S(1)} fusion(s32[8192]{0:T(1024)S(1)} %dynamic_slice.21, s32[512]{0:T(512)} %bitcast.36, bf16[64,65536]{1,0:T(8,128)(2,1)} %get-tuple-element.220, s32[]{:T(128)S(6)} %select_n.101, f32[64,512]{1,0:T(8,128)S(1)} %get-tuple-element.208, pred[]{:T(512)S(6)} %compare.11), kind=kOutput, calls=%fused_computation.9.clone.1 | convolution fusion | flops 541130752 | bytes 1345541 | tf_op jit(solution)/shard_map/while/body/eval_jaxpr/dot_general | solution.py:56
  36.3 2.5 %convert_reduce_fusion.4 = f32[512]{0:T(512)S(1)} fusion(s32[8192]{0:T(1024)S(1)} %dynamic_slice.21, s32[512]{0:T(512)} %bitcast.37), kind=kLoop, calls=%fused_computation.6.clone.1 | loop fusion | flops 16776704 | bytes 36864 | tf_op jit(solution)/shard_map/while/body/eval_jaxpr/reduce_sum | solution.py:59
  39.5 4.3 %fusion.21 = f32[64,512]{1,0:T(8,128)S(1)} fusion(s32[8192]{0:T(1024)S(1)} %dynamic_slice.21, s32[512]{0:T(512)} %bitcast.36, bf16[64,65536]{1,0:T(8,128)(2,1)} %get-tuple-element.220, s32[]{:T(128)S(6)} %select_n.101, f32[64,512]{1,0:T(8,128)S(1)} %get-tuple-element.208, pred[]{:T(512)S(6)} %compare.11), kind=kOutput, calls=%fused_computation.9.clone.1 | convolution fusion | flops 541130752 | bytes 1345541 | tf_op jit(solution)/shard_map/while/body/eval_jaxpr/dot_general | solution.py:56
  43.8 2.5 %convert_reduce_fusion.4 = f32[512]{0:T(512)S(1)} fusion(s32[8192]{0:T(1024)S(1)} %dynamic_slice.21, s32[512]{0:T(512)} %bitcast.37), kind=kLoop, calls=%fused_computation.6.clone.1 | loop fusion | flops 16776704 | bytes 36864 | tf_op jit(solution)/shard_map/while/body/eval_jaxpr/reduce_sum | solution.py:59
  47.1 4.3 %fusion.21 = f32[64,512]{1,0:T(8,128)S(1)} fusion(s32[8192]{0:T(1024)S(1)} %dynamic_slice.21, s32[512]{0:T(512)} %bitcast.36, bf16[64,65536]{1,0:T(8,128)(2,1)} %get-tuple-element.220, s32[]{:T(128)S(6)} %select_n.101, f32[64,512]{1,0:T(8,128)S(1)} %get-tuple-element.208, pred[]{:T(512)S(6)} %compare.11), kind=kOutput, calls=%fused_computation.9.clone.1 | convolution fusion | flops 541130752 | bytes 1345541 | tf_op jit(solution)/shard_map/while/body/eval_jaxpr/dot_general | solution.py:56
  51.3 2.5 %convert_reduce_fusion.4 = f32[512]{0:T(512)S(1)} fusion(s32[8192]{0:T(1024)S(1)} %dynamic_slice.21, s32[512]{0:T(512)} %bitcast.37), kind=kLoop, calls=%fused_computation.6.clone.1 | loop fusion | flops 16776704 | bytes 36864 | tf_op jit(solution)/shard_map/while/body/eval_jaxpr/reduce_sum | solution.py:59
  53.8 0.8 dynamic_slice.21
  54.6 4.3 %fusion.21 = f32[64,512]{1,0:T(8,128)S(1)} fusion(s32[8192]{0:T(1024)S(1)} %dynamic_slice.21, s32[512]{0:T(512)} %bitcast.36, bf16[64,65536]{1,0:T(8,128)(2,1)} %get-tuple-element.220, s32[]{:T(128)S(6)} %select_n.101, f32[64,512]{1,0:T(8,128)S(1)} %get-tuple-element.208, pred[]{:T(512)S(6)} %compare.11), kind=kOutput, calls=%fused_computation.9.clone.1 | convolution fusion | flops 541130752 | bytes 1345541 | tf_op jit(solution)/shard_map/while/body/eval_jaxpr/dot_general | solution.py:56
  58.9 2.5 %convert_reduce_fusion.4 = f32[512]{0:T(512)S(1)} fusion(s32[8192]{0:T(1024)S(1)} %dynamic_slice.21, s32[512]{0:T(512)} %bitcast.37), kind=kLoop, calls=%fused_computation.6.clone.1 | loop fusion | flops 16776704 | bytes 36864 | tf_op jit(solution)/shard_map/while/body/eval_jaxpr/reduce_sum | solution.py:59
  61.5 2.8 %gather_fusion = f32[1024,64]{1,0:T(8,128)S(1)} fusion(f32[64,512]{0,1:T(8,128)S(1)} %copy.34, s32[1024]{0:T(1024)S(1)} %broadcast_clamp_fusion), kind=kCustom, calls=%fused_computation | custom fusion | bytes 528384 | tf_op jit(solution)/shard_map/jit(_take)/gather | solution.py:76
  64.7 6.9 %gather_fusion.1 = f32[1024]{0:T(1024)S(1)} fusion(f32[512]{0:T(512)S(1)} %get-tuple-element.116, s32[1024]{0:T(1024)S(1)} %broadcast_clamp_fusion), kind=kCustom, calls=%fused_computation.1 | custom fusion | bytes 12288 | tf_op jit(solution)/shard_map/jit(_take)/gather | solution.py:79
  71.7 6.9 %gather_fusion.2 = s32[1024]{0:T(1024)S(1)} fusion(s32[512]{0:T(512)S(1)} %get-tuple-element.155, s32[1024]{0:T(1024)S(1)} %broadcast_clamp_fusion), kind=kCustom, calls=%fused_computation.2 | custom fusion | bytes 12288 | tf_op jit(solution)/shard_map/jit(_take)/gather | solution.py:83
  79.1 25.4 %all_to_all.18 = f32[64,1,1056]{2,1,0:T(1,128)S(1)} all-to-all(f32[64,1,1056]{2,1,0:T(1,128)S(1)} %copy.38), channel_id=1, replica_groups=mesh['grp'=4,'dev'=64] {'dev'}, dimensions={0} | all-to-all | bytes 540672 | tf_op jit(solution)/shard_map/all_to_all | solution.py:16
  107.0 9.8 %all_to_all.19 = f32[4,1,16640]{2,1,0:T(1,128)S(1)} all-to-all(f32[4,1,16640]{2,1,0:T(1,128)S(1)} %broadcast_in_dim.74), channel_id=1, replica_groups=mesh['grp'=4,'dev'=64] {'grp'}, dimensions={0} | all-to-all | bytes 532480 | tf_op jit(solution)/shard_map/all_to_all | solution.py:23
  (52 shorter events, 10.1 us)
where the time goes:
time: 119 us; the launch traced here: 118 us
  matrix products  35.3 us (30%)
  blocking collectives  35.2 us (30%)
  local copies, waits for them, and re-layouts  25 us (21%)
  other arithmetic  21.8 us (18%)
    dot_general x8, matrix products, accumulate(): lax.dot_general(block_values, one_hot, (((1,), (1,)), ((), ())), preferre...  34.1 us
    all_to_all x1, blocking collectives, sent_together(): lax.all_to_all(both, axis, split_axis=split_dim, concat_axis=concat_dim,...  25.4 us
    reduce_sum x8, other arithmetic, accumulate(): jnp.sum(one_hot, axis=1, dtype=jnp.float32)  19.8 us
    all_to_all x1, blocking collectives, copy_for_each(): return lax.all_to_all(copies, axis, split_axis=0, concat_axis=0, tiled=True)  9.82 us
    gather x3, local copies, waits for them, and re-layouts, body(): jnp.take(local_place, source_slot).reshape(owner_count, capacity)  7.03 us
    gather x3, local copies, waits for them, and re-layouts, body(): jnp.take(partial_counts, source_slot).reshape(owner_count, capacity)  7.02 us
    dynamic_slice x8, local copies, waits for them, and re-layouts, accumulate(): lax.dynamic_slice_in_dim(label_row, block_index * block_size, block_size)  6.12 us
    gather x2, local copies, waits for them, and re-layouts, body(): jnp.take(partial_sums, source_slot, axis=1)  3.18 us

commit v1 on v0

v1 whole, which is shorter than its diff:
```python
import functools

import jax
import jax.numpy as jnp
from jax import lax
from jax.experimental import pallas as pl
from jax.experimental.pallas import tpu as pltpu
from jax.sharding import PartitionSpec as P

ZONES = 16384
RANGE = 256
CAP = 16
CHUNKS = 8
F32, BF16, F8, I32 = jnp.float32, jnp.bfloat16, jnp.float8_e4m3fn, jnp.int32
MESH = pl.DeviceIdType.MESH
VMEM = pl.BlockSpec(memory_space=pltpu.VMEM)
ANY = pl.BlockSpec(memory_space=pl.ANY)
VMEM_ALL = 67043328


def nt(a, b):
    return lax.dot_general(a, b, (((1,), (1,)), ((), ())), preferred_element_type=F32)


def nn(a, b):
    return lax.dot_general(a, b, (((1,), (0,)), ((), ())), preferred_element_type=F32)


def onehot(mask, dtype=BF16):
    return jnp.where(mask, 1.0, 0.0).astype(dtype)


def two_parts(x):
    high = x.astype(BF16)
    return high, (x - high.astype(F32)).astype(BF16)


def lookup(table, word):
    row, lane = word >> 7, word & 127
    out = jnp.zeros_like(word)
    for a in range(8):
        source = jnp.broadcast_to(table[a : a + 1, :], word.shape)
        out = jnp.where(row == a, jnp.take_along_axis(source, lane, axis=1), out)
    return out


def table_kernel(present_ref, table_ref, slot_ref):
    present = present_ref[...]
    row8 = lax.broadcasted_iota(I32, (8, 128), 0)
    row128 = lax.broadcasted_iota(I32, (128, 128), 0)
    bitmap = jnp.zeros((8, 128), F32)
    prefix = jnp.zeros((8, 128), F32)
    ones = jnp.ones((128, 128), BF16)
    for c in range(4):
        zone = present[c : c + 1, :]
        top = jnp.broadcast_to(zone >> 11, (8, 128))
        middle = jnp.broadcast_to((zone >> 4) & 127, (128, 128))
        power = (jnp.full_like(zone, 1) << (zone & 15)).astype(F32)
        weight = jnp.where(top == row8, jnp.broadcast_to(power, (8, 128)), 0.0).astype(BF16)
        bitmap += nt(weight, onehot(middle == row128))
        prefix += nt(onehot(top == row8), onehot(middle < row128)) + nt(onehot(top < row8), ones)
    table = (prefix.astype(I32) << 16) | bitmap.astype(I32)
    table_ref[...] = table
    first = lookup(table, (present >> 8) << 4) >> 16
    place = lax.broadcasted_iota(I32, present.shape, 0) * 128 + lax.broadcasted_iota(I32, present.shape, 1)
    slot_ref[...] = place - first


def rank_of(labels, table):
    entry = lookup(table, labels >> 4)
    bit = labels & 15
    below = (jnp.full_like(bit, 1) << bit) - 1
    rank = (entry >> 16) + lax.population_count(entry & 65535 & below)
    listed = ((entry >> bit) & 1) == 1
    return rank & 255, jnp.where(listed, rank >> 8, 8)


def sums_kernel(table_ref, labels_ref, values_ref, out_ref, buf, lo_ref, hi_ref, sems):
    width = buf.shape[2]
    steps = width // 256

    def chunk_copy(k):
        return pltpu.make_async_copy(
            values_ref.at[:, pl.ds(pl.multiple_of(k * width, width), width)], buf.at[k], sems.at[k]
        )

    for k in range(CHUNKS):
        chunk_copy(k).start()
    table = table_ref[...]

    @pl.loop(0, lo_ref.shape[0] // 64)
    def _(i):
        rows = pl.ds(pl.multiple_of(i * 64, 64), 64)
        labels = labels_ref[rows, :]
        low, high = [], []
        for k in range(8):
            a, b = rank_of(labels[8 * k : 8 * k + 8], table)
            low.append(a)
            high.append(b)
        lo_ref[rows, :] = jnp.concatenate(low, 0).astype(F32)
        hi_ref[rows, :] = jnp.concatenate(high, 0).astype(F32)

    def run(*refs):
        accs = (refs[:3], refs[3:])
        for q in range(2):
            for a in accs[q]:
                pltpu.matmul_pop(a)
        row256 = lax.broadcasted_iota(I32, (256, 128), 0).astype(F32).astype(BF16)
        row16 = lax.broadcasted_iota(I32, (16, 128), 0).astype(F32).astype(BF16)
        one, zero = jnp.ones((), BF16), jnp.zeros((), BF16)

        @pl.loop(0, CHUNKS)
        def _(k):
            chunk_copy(k).wait()
            for j in range(steps):
                q, reg = j % 2, (j // 2) % 2
                hots, first, second, marks = [], [], [], []
                for s in range(2):
                    row = k * (width // 128) + 2 * j + s
                    low = jnp.broadcast_to(lo_ref[pl.ds(row, 1), :], (16, 128)).astype(BF16)
                    high = jnp.broadcast_to(hi_ref[pl.ds(row, 1), :], (16, 128)).astype(BF16)
                    hots.append(jnp.where(jnp.tile(low, (16, 1)) == row256, one, zero).astype(F8))
                    pixels = buf[k, :, pl.ds(256 * j + 128 * s, 128)]
                    high64 = jnp.tile(high, (4, 1))
                    first.append(jnp.where(high64 == zero, pixels, zero))
                    second.append(jnp.where(high64 == one, pixels, zero))
                    marks.append(jnp.where(high == row16, one, zero))
                joined = [jnp.concatenate(p, 1) for p in (hots, first, second, marks)]
                pltpu.matmul_push_rhs(joined[0], staging_register=reg, mxu_index=q, transpose=True)
                pltpu.matmul_acc_lhs(accs[q][0], joined[1], load_staged_rhs=reg)
                pltpu.matmul_acc_lhs(accs[q][1], joined[2])
                pltpu.matmul_acc_lhs(accs[q][2], joined[3])

        for a, b, at, rows in zip(accs[0], accs[1], (0, 64, 128), (64, 64, 16)):
            out_ref[at : at + rows, :] = pltpu.matmul_pop(a) + pltpu.matmul_pop(b)

    specs = []
    for q in range(2):
        specs += [pltpu.ACC(q)((rows, 256), F32) for rows in (64, 64, 16)]
    pl.run_scoped(run, *specs)


def pick_kernel(owners, present_ref, slot_ref, sums_ref, me_ref, tiles_ref, places_ref, counts_ref):
    present = present_ref[...]
    slot = slot_ref[...]
    total = jnp.zeros((owners * 8, 256), F32)
    places = jnp.zeros((owners, 128), F32)
    counts = jnp.zeros((owners, 128), F32)
    owner_row = lax.broadcasted_iota(I32, (owners, 256), 0)
    pair_row = lax.broadcasted_iota(I32, (owners * 8, 256), 0)
    lane_row = lax.broadcasted_iota(I32, (128, 256), 0)
    shift = (me_ref[0] & 7) * CAP
    empty = jnp.zeros((64, 256), BF16)
    for h in range(2):
        zone = jnp.concatenate([present[2 * h : 2 * h + 1], present[2 * h + 1 : 2 * h + 2]], 1)
        at = jnp.concatenate([slot[2 * h : 2 * h + 1], slot[2 * h + 1 : 2 * h + 2]], 1)
        owner = zone >> 8
        place = (owner << 3) + (at & 7)
        place_b = jnp.broadcast_to(place, (owners * 8, 256))
        parity_b = jnp.broadcast_to(at >> 3, (owners * 8, 256))
        high, rest = two_parts(sums_ref[64 * h : 64 * h + 64, :])
        for parity in range(2):
            pick = onehot((place_b == pair_row) & (parity_b == parity))
            order = (high, empty, rest, empty) if parity == 0 else (empty, high, empty, rest)
            total += nt(pick, jnp.concatenate(order, 0))
        mine = jnp.broadcast_to(owner, (owners, 256)) == owner_row
        lanes = onehot(jnp.broadcast_to(at, (128, 256)) + shift == lane_row)
        number = jnp.broadcast_to(((zone & 255) + 1).astype(F32), (owners, 256))
        places += nt(jnp.where(mine, number, 0.0).astype(BF16), lanes)
        for part in two_parts(sums_ref[128 + h : 129 + h, :]):
            spread = jnp.broadcast_to(part.astype(F32), (owners, 256))
            counts += nt(jnp.where(mine, spread, 0.0).astype(BF16), lanes)
    tiles_ref[...] = (total[:, :128] + total[:, 128:]).reshape(owners, 8, 128)
    places_ref[:, 0, :] = places
    counts_ref[:, 0, :] = counts


def exchange_kernel(
    owners, groups, tiles_ref, places_ref, counts_ref, out_ref,
    got_tiles, got_places, got_counts, ours, theirs, send_sems, recv_sems, y_send, y_recv,
):
    g, me = lax.axis_index("grp"), lax.axis_index("dev")
    barrier = pltpu.get_barrier_semaphore()

    @pl.loop(1, owners)
    def _(k):
        pl.semaphore_signal(barrier, inc=1, device_id=(g, lax.rem(me + k, owners)), device_id_type=MESH)

    @pl.loop(1, groups)
    def _(k):
        pl.semaphore_signal(barrier, inc=1, device_id=(lax.rem(g + k, groups), me), device_id_type=MESH)

    pl.semaphore_wait(barrier, owners + groups - 2)
    pairs = ((tiles_ref, got_tiles), (places_ref, got_places), (counts_ref, got_counts))

    @pl.loop(1, owners)
    def _(k):
        to = lax.rem(me + k, owners)
        for n, (source, landing) in enumerate(pairs):
            pltpu.make_async_remote_copy(
                src_ref=source.at[to], dst_ref=landing.at[me], send_sem=send_sems.at[n],
                recv_sem=recv_sems.at[n], device_id=(g, to), device_id_type=MESH,
            ).start()

    for source, landing in pairs:
        landing[me] = source[me]
    for n, (source, landing) in enumerate(pairs):
        whole = pltpu.make_async_remote_copy(
            src_ref=source.at[pl.ds(0, owners - 1)], dst_ref=landing.at[pl.ds(0, owners - 1)],
            send_sem=send_sems.at[n], recv_sem=recv_sems.at[n],
            device_id=(g, lax.rem(me + 1, owners)), device_id_type=MESH,
        )
        whole.wait_recv()
        whole.wait_send()

    place = jnp.sum(got_places[:, 0, :].reshape(owners // 8, 8, 128), axis=1)
    count = jnp.sum(got_counts[:, 0, :].reshape(owners // 8, 8, 128), axis=1)
    number = lax.broadcasted_iota(I32, (RANGE, 128), 0).astype(F32) + 1.0
    lane = lax.broadcasted_iota(I32, (8, 8, 128), 2)
    first_row = lax.broadcasted_iota(I32, (16, 128), 0)
    sums = jnp.zeros((RANGE, 256), F32)
    counted = jnp.zeros((16, RANGE), F32)
    for i in range(owners // 8):
        put = onehot(jnp.broadcast_to(place[i : i + 1], (RANGE, 128)) == number)
        tiles = got_tiles[8 * i : 8 * i + 8]
        split = jnp.stack([jnp.where(lane < 64, tiles, 0.0), jnp.where(lane < 64, 0.0, tiles)], 1)
        sums += nn(put, jnp.concatenate(two_parts(split.reshape(128, 128)), 1))
        high, rest = (jnp.broadcast_to(p.astype(F32), (16, 128)) for p in two_parts(count[i : i + 1]))
        marks = jnp.where(first_row == 0, high, jnp.where(first_row == 1, rest, 0.0))
        counted += nt(marks.astype(BF16), put)
    both = (sums[:, :128] + sums[:, 128:]).T
    ours[0:64] = both[:64] + both[64:]
    ours[64:72] = jnp.broadcast_to(counted[0:1] + counted[1:2], (8, RANGE))

    @pl.loop(1, groups)
    def _(k):
        to = lax.rem(g + k, groups)
        pltpu.make_async_remote_copy(
            src_ref=ours, dst_ref=theirs.at[k - 1], send_sem=y_send.at[k - 1], recv_sem=y_recv.at[k - 1],
            device_id=(to, me), device_id_type=MESH,
        ).start()

    total = ours[...]
    for k in range(1, groups):
        copy = pltpu.make_async_remote_copy(
            src_ref=ours, dst_ref=theirs.at[k - 1], send_sem=y_send.at[k - 1], recv_sem=y_recv.at[k - 1],
            device_id=(lax.rem(g + k, groups), me), device_id_type=MESH,
        )
        copy.wait_recv()
        total = total + theirs[k - 1]
    for k in range(1, groups):
        pltpu.make_async_remote_copy(
            src_ref=ours, dst_ref=theirs.at[k - 1], send_sem=y_send.at[k - 1], recv_sem=y_recv.at[k - 1],
            device_id=(lax.rem(g + k, groups), me), device_id_type=MESH,
        ).wait_send()
    out_ref[...] = total


def shaped(shape, dtype=F32):
    return jax.ShapeDtypeStruct(shape, dtype)


def local_sums(table, labels, values):
    times, pixels = values.shape
    return pl.pallas_call(
        sums_kernel,
        out_shape=shaped((144, 256)),
        in_specs=[VMEM, VMEM, ANY],
        out_specs=VMEM,
        scratch_shapes=[
            pltpu.VMEM((CHUNKS, times, pixels // CHUNKS), BF16),
            pltpu.VMEM((pixels // 128, 128), F32),
            pltpu.VMEM((pixels // 128, 128), F32),
            pltpu.SemaphoreType.DMA((CHUNKS,)),
        ],
        compiler_params=pltpu.CompilerParams(vmem_limit_bytes=VMEM_ALL),
    )(table, labels.reshape(pixels // 128, 128), values)


def exchange(owners, groups, tiles, places, counts):
    return pl.pallas_call(
        functools.partial(exchange_kernel, owners, groups),
        out_shape=shaped((72, RANGE)),
        in_specs=[VMEM, VMEM, VMEM],
        out_specs=VMEM,
        scratch_shapes=[
            pltpu.VMEM((owners, 8, 128), F32),
            pltpu.VMEM((owners, 1, 128), F32),
            pltpu.VMEM((owners, 1, 128), F32),
            pltpu.VMEM((72, RANGE), F32),
            pltpu.VMEM((groups - 1, 72, RANGE), F32),
            pltpu.SemaphoreType.DMA((3,)),
            pltpu.SemaphoreType.DMA((3,)),
            pltpu.SemaphoreType.DMA((groups - 1,)),
            pltpu.SemaphoreType.DMA((groups - 1,)),
        ],
        compiler_params=pltpu.CompilerParams(collective_id=0, has_side_effects=True),
    )(tiles, places, counts)


def body(labels, present, values):
    owners, groups = lax.axis_size("dev"), lax.axis_size("grp")
    listed = present.reshape(4, 128)
    table, slot = pl.pallas_call(
        table_kernel, out_shape=(shaped((8, 128), I32), shaped((4, 128), I32)),
        in_specs=[VMEM], out_specs=(VMEM, VMEM),
    )(listed)
    sums = local_sums(table, labels, values[0])
    me = lax.axis_index("dev").astype(I32).reshape(1)
    tiles, places, counts = pl.pallas_call(
        functools.partial(pick_kernel, owners),
        out_shape=(shaped((owners, 8, 128)), shaped((owners, 1, 128)), shaped((owners, 1, 128))),
        in_specs=[VMEM, VMEM, VMEM, pl.BlockSpec(memory_space=pltpu.SMEM)],
        out_specs=(VMEM, VMEM, VMEM),
    )(listed, slot, sums, me)
    total = exchange(owners, groups, tiles, places, counts)
    return total[:64] / jnp.maximum(total[64:65], 1.0)


def solution(mesh):
    return jax.shard_map(
        body,
        mesh=mesh,
        in_specs=(P(("grp", "dev"), None), P(("grp", "dev"), None), P(("grp", "dev"), None, None)),
        out_specs=P(None, "dev"),
        check_vma=False,
    )
```

time: 119 us -> 44.7 us (0.38)
  Pallas kernels: 0 us -> 42.2 us
  matrix products: 35.3 us -> 0 us
  blocking collectives: 35.2 us -> 0 us
  local copies, waits for them, and re-layouts: 25 us -> 0 us
  other arithmetic: 21.8 us -> 2.18 us
    pallas_call x0 -> x4, Pallas kernels: none -> 42.2 us  [the longest x1 29.6 us: exchange(): pl.pallas_call(functools.partial(exchange_kernel, owners, groups), out_sh...]
    dot_general x10 -> x0, matrix products: 35.3 us -> none  [the longest x8 34.1 us: accumulate(): lax.dot_general(block_values, one_hot, (((1,), (1,)), ((), ())), preferre...]
    all_to_all x2 -> x0, blocking collectives: 35.2 us -> none  [the longest x1 25.4 us: sent_together(): lax.all_to_all(both, axis, split_axis=split_dim, concat_axis=concat_dim,...]
    reduce_sum x10 -> x0, other arithmetic: 20.2 us -> none  [the longest x8 19.8 us: accumulate(): jnp.sum(one_hot, axis=1, dtype=jnp.float32)]
    gather x8 -> x0, local copies, waits for them, and re-layouts: 17.2 us -> none  [the longest x3 7.03 us: body(): jnp.take(local_place, source_slot).reshape(owner_count, capacity)]
    dynamic_slice x8 -> x0, local copies, waits for them, and re-layouts: 6.12 us -> none  [accumulate(): lax.dynamic_slice_in_dim(label_row, block_index * block_size, block_size)]
where the time goes in v1:
time: 44.7 us; the launch traced here: 44.4 us
  Pallas kernels  42.2 us (94%)
  other arithmetic  2.18 us (5%)
    pallas_call x1, Pallas kernels, exchange(): pl.pallas_call(functools.partial(exchange_kernel, owners, groups), out_sh...  29.6 us
    pallas_call x1, Pallas kernels, local_sums(): pl.pallas_call(sums_kernel, out_shape=shaped((144, 256)), in_specs=[VMEM,...  8.78 us
    pallas_call x1, Pallas kernels, body(): pl.pallas_call(functools.partial(pick_kernel, owners), out_shape=(shaped(...  2.22 us
    pallas_call x1, Pallas kernels, body(): pl.pallas_call(table_kernel, out_shape=(shaped((8, 128), I32), shaped((4,...  1.67 us
    div x1, other arithmetic, body(): return total[:64] / jnp.maximum(total[64:65], 1.0)  1.48 us

profile of v1, /device:TPU:1, one launch (start us, length us, event | category | flops | bytes accessed | tf_op | source)
XLA Modules:
  0.0 44.4 jit_solution(9848096027167612667)
XLA Ops:
  0.0 1.7 %shard_map.37 = (s32[8,128]{1,0:T(8,128)}, s32[4,128]{1,0:T(4,128)}) custom-call(s32[4,128]{1,0:T(4,128)} %bitcast.7), custom_call_target="tpu_custom_call" | custom-call | tf_op jit(solution)/shard_map/pallas_call | solution.py:304
  1.7 8.8 %shard_map.38.sums_ref = f32[144,256]{1,0:T(8,128)} custom-call(s32[8,128]{1,0:T(8,128)} %get-tuple-element.11.table_ref, s32[512,128]{1,0:T(8,128)} %bitcast.6, bf16[64,65536]{1,0:T(8,128)(2,1)} %bitcast.5), custom_call_target="tpu_custom_call" | custom-call | tf_op jit(solution)/shard_map/pallas_call | solution.py:265
  10.5 2.2 %shard_map.39 = (f32[64,8,128]{2,1,0:T(8,128)}, f32[64,1,128]{2,1,0:T(1,128)}, f32[64,1,128]{2,1,0:T(1,128)}) custom-call(s32[4,128]{1,0:T(4,128)} %bitcast.8, s32[4,128]{1,0:T(4,128)} %get-tuple-element.10.slot_ref, f32[144,256]{1,0:T(8,128)} %shard_map.38.sums_ref, s32[1]{0:T(128)} %bitcast.3.me_ref), custom_call_target="tpu_custom_call" | custom-call | tf_op jit(solution)/shard_map/pallas_call | solution.py:310
  12.7 29.6 %shard_map.40 = f32[72,256]{1,0:T(8,128)} custom-call(f32[64,8,128]{2,1,0:T(8,128)} %get-tuple-element.12.tiles_ref, f32[64,1,128]{2,1,0:T(1,128)} %get-tuple-element.13.places_ref, f32[64,1,128]{2,1,0:T(1,128)} %get-tuple-element.14.counts_ref), custom_call_target="tpu_custom_call" | custom-call | tf_op jit(solution)/shard_map/pallas_call | solution.py:281
  42.2 0.7 %slice_maximum_fusion = f32[1,256]{1,0:T(1,128)S(1)} fusion(f32[72,256]{1,0:T(8,128)} %shard_map.40), kind=kLoop, calls=%fused_computation.1 | loop fusion | flops 256 | bytes 2048 | tf_op jit(solution)/shard_map/max | solution.py:317
  42.9 1.5 %slice_divide_fusion = f32[64,256]{1,0:T(8,128)} fusion(f32[72,256]{1,0:T(8,128)} %shard_map.40, f32[256]{0:T(256)S(1)} %bitcast.9), kind=kLoop, calls=%fused_computation | loop fusion | flops 16384 | bytes 132096 | tf_op jit(solution)/shard_map/div | solution.py:317

commit v2 on v0

v2 whole, which is shorter than its diff:
```python
import functools

import jax
import jax.numpy as jnp
from jax import lax
from jax.experimental import pallas as pl
from jax.experimental.pallas import tpu as pltpu
from jax.sharding import PartitionSpec as P

ZONES = 16384
RANGE = 256
CAP = 16
CHUNKS = 8
F32, BF16, F8, I32 = jnp.float32, jnp.bfloat16, jnp.float8_e4m3fn, jnp.int32
MESH = pl.DeviceIdType.MESH
VMEM = pl.BlockSpec(memory_space=pltpu.VMEM)
ANY = pl.BlockSpec(memory_space=pl.ANY)
VMEM_ALL = 67043328


def onehot(mask, dtype=BF16):
    return jnp.where(mask, 1.0, 0.0).astype(dtype)


def two_parts(x):
    high = x.astype(BF16)
    return high, (x - high.astype(F32)).astype(BF16)


def lookup(table, word):
    row, lane = word >> 7, word & 127
    out = jnp.zeros_like(word)
    for a in range(8):
        source = jnp.broadcast_to(table[a : a + 1, :], word.shape)
        out = jnp.where(row == a, jnp.take_along_axis(source, lane, axis=1), out)
    return out


def rank_of(labels, table):
    entry = lookup(table, labels >> 4)
    bit = labels & 15
    below = (jnp.full_like(bit, 1) << bit) - 1
    rank = (entry >> 16) + lax.population_count(entry & 65535 & below)
    listed = ((entry >> bit) & 1) == 1
    return rank & 255, jnp.where(listed, rank >> 8, 8)


def wide(row, rows):
    return jnp.broadcast_to(row, (rows, row.shape[1]))


def beside(ref_value, h):
    return jnp.concatenate([ref_value[2 * h : 2 * h + 1], ref_value[2 * h + 1 : 2 * h + 2]], 1)


def make_table(present, accs):
    row8 = lax.broadcasted_iota(I32, (8, 256), 0)
    row128 = lax.broadcasted_iota(I32, (128, 256), 0)
    below = jnp.zeros((8, 1), F32)
    for h in range(2):
        zone = beside(present, h)
        top = wide(zone >> 11, 8)
        middle = wide((zone >> 4) & 127, 128)
        power = (jnp.full_like(zone, 1) << (zone & 15)).astype(F32)
        left = jnp.concatenate(
            [jnp.where(top == row8, wide(power, 8), 0.0), jnp.where(top == row8, 1.0, 0.0)], 0
        ).astype(BF16)
        right = jnp.concatenate([onehot(middle == row128), onehot(middle < row128)], 0)
        pltpu.matmul_push_rhs(right, staging_register=0, mxu_index=h, transpose=True)
        pltpu.matmul_acc_lhs(accs[h], left, load_staged_rhs=0)
        below += jnp.sum(jnp.where(top < row8, 1.0, 0.0), axis=1, keepdims=True)
    both = pltpu.matmul_pop(accs[0]) + pltpu.matmul_pop(accs[1])
    prefix = both[8:16, 128:256] + below
    return (prefix.astype(I32) << 16) | both[0:8, 0:128].astype(I32)


def fused_kernel(
    owners, groups, present_ref, labels_ref, values_ref, out_ref,
    buf, lab_ref, lo_ref, hi_ref, slot_ref, sums_ref, tiles_ref, places_ref, counts_ref,
    got_tiles, got_places, got_counts, ours, theirs,
    in_sems, lab_sem, send_sems, recv_sems, y_send, y_recv,
):
    g, me = lax.axis_index("grp"), lax.axis_index("dev")
    width = buf.shape[2]
    steps = width // 256
    one, zero = jnp.ones((), BF16), jnp.zeros((), BF16)

    def chunk_copy(k):
        return pltpu.make_async_copy(
            values_ref.at[:, pl.ds(pl.multiple_of(k * width, width), width)], buf.at[k], in_sems.at[k]
        )

    lab_copy = pltpu.make_async_copy(labels_ref, lab_ref, lab_sem)
    lab_copy.start()
    for k in range(CHUNKS):
        chunk_copy(k).start()

    barrier = pltpu.get_barrier_semaphore()

    @pl.loop(1, owners)
    def _(k):
        pl.semaphore_signal(barrier, inc=1, device_id=(g, lax.rem(me + k, owners)), device_id_type=MESH)

    @pl.loop(1, groups)
    def _(k):
        pl.semaphore_signal(barrier, inc=1, device_id=(lax.rem(g + k, groups), me), device_id_type=MESH)

    present = present_ref[...]
    owner_row = lax.broadcasted_iota(I32, (owners, 256), 0)
    lane_row = lax.broadcasted_iota(I32, (256, 256), 0)
    shift = (me & 7) * CAP

    def clear(*accs):
        for a in accs:
            pltpu.matmul_pop(a)

    pl.run_scoped(clear, *[pltpu.ACC(q)((1024, 256), F32) for q in range(2)])

    def prepare(*accs):
        table = make_table(present, accs[:2])
        first = lookup(table, (present >> 8) << 4) >> 16
        index = lax.broadcasted_iota(I32, present.shape, 0) * 128 + lax.broadcasted_iota(I32, present.shape, 1)
        slot = index - first
        for h in range(2):
            zone, at = beside(present, h), beside(slot, h)
            mine = wide(zone >> 8, owners) == owner_row
            lanes = onehot(wide(at, 256) + shift == lane_row)
            number = wide(((zone & 255) + 1).astype(F32), owners)
            pltpu.matmul_push_rhs(lanes, staging_register=0, mxu_index=h, transpose=True)
            pltpu.matmul_acc_lhs(accs[2 + h], jnp.where(mine, number, 0.0).astype(BF16), load_staged_rhs=0)
        places_ref[:, 0, :] = (pltpu.matmul_pop(accs[2]) + pltpu.matmul_pop(accs[3]))[:, :128]
        lab_copy.wait()

        @pl.loop(0, lo_ref.shape[0] // 64)
        def _(i):
            rows = pl.ds(pl.multiple_of(i * 64, 64), 64)
            labels = lab_ref[rows, :]
            low, high = [], []
            for k in range(8):
                a, b = rank_of(labels[8 * k : 8 * k + 8], table)
                low.append(a)
                high.append(b)
            lo_ref[rows, :] = jnp.concatenate(low, 0).astype(F32)
            hi_ref[rows, :] = jnp.concatenate(high, 0).astype(F32)

        slot_ref[...] = slot

    pl.run_scoped(prepare, *[pltpu.ACC(q)((rows, 256), F32) for rows in (16, owners) for q in range(2)])

    def send(n, source, landing, k):
        to = lax.rem(me + k, owners)
        pltpu.make_async_remote_copy(
            src_ref=source.at[to], dst_ref=landing.at[me], send_sem=send_sems.at[n],
            recv_sem=recv_sems.at[n], device_id=(g, to), device_id_type=MESH,
        ).start()

    def add_up(*refs):
        accs = (refs[:3], refs[3:])
        row256 = lax.broadcasted_iota(I32, (256, 128), 0).astype(F32).astype(BF16)
        row16 = lax.broadcasted_iota(I32, (16, 128), 0).astype(F32).astype(BF16)

        def chunk(k):
            chunk_copy(k).wait()
            for j in range(steps):
                q, reg = j % 2, (j // 2) % 2
                hots, first, second, marks = [], [], [], []
                for s in range(2):
                    row = k * (width // 128) + 2 * j + s
                    low = wide(lo_ref[pl.ds(row, 1), :], 16).astype(BF16)
                    high = wide(hi_ref[pl.ds(row, 1), :], 16).astype(BF16)
                    hots.append(jnp.where(jnp.tile(low, (16, 1)) == row256, one, zero).astype(F8))
                    pixels = buf[k, :, pl.ds(256 * j + 128 * s, 128)]
                    high64 = jnp.tile(high, (4, 1))
                    first.append(jnp.where(high64 == zero, pixels, zero))
                    second.append(jnp.where(high64 == one, pixels, zero))
                    marks.append(jnp.where(high == row16, one, zero))
                joined = [jnp.concatenate(p, 1) for p in (hots, first, second, marks)]
                pltpu.matmul_push_rhs(joined[0], staging_register=reg, mxu_index=q, transpose=True)
                pltpu.matmul_acc_lhs(accs[q][0], joined[1], load_staged_rhs=reg)
                pltpu.matmul_acc_lhs(accs[q][1], joined[2])
                pltpu.matmul_acc_lhs(accs[q][2], joined[3])

        pl.loop(0, CHUNKS - 2)(chunk)
        pl.semaphore_wait(barrier, owners + groups - 2)
        pl.loop(1, owners)(functools.partial(send, 0, places_ref, got_places))
        pl.loop(CHUNKS - 2, CHUNKS)(chunk)
        for a, b, at, rows in zip(accs[0], accs[1], (0, 64, 128), (64, 64, 16)):
            sums_ref[at : at + rows, :] = pltpu.matmul_pop(a) + pltpu.matmul_pop(b)

    pl.run_scoped(add_up, *[pltpu.ACC(q)((rows, 256), F32) for q in range(2) for rows in (64, 64, 16)])

    def pick_slots(*accs):
        slot = slot_ref[...]
        pair_row = lax.broadcasted_iota(I32, (owners * 8, 256), 0)
        empty = jnp.zeros((64, 256), BF16)
        for h in range(2):
            zone, at = beside(present, h), beside(slot, h)
            owner = zone >> 8
            target = ((owner << 3) + (at & 7)) * 2 + (at >> 3)
            high, rest = two_parts(sums_ref[64 * h : 64 * h + 64, :])
            for parity in range(2):
                order = (high, empty, rest, empty) if parity == 0 else (empty, high, empty, rest)
                pltpu.matmul_push_rhs(
                    jnp.concatenate(order, 0), staging_register=h, mxu_index=parity, transpose=True
                )
                pick = onehot(wide(target, owners * 8) == pair_row * 2 + parity)
                pltpu.matmul_acc_lhs(accs[parity], pick, load_staged_rhs=h)
            mine = wide(owner, owners) == owner_row
            lanes = onehot(wide(at, 256) + shift == lane_row)
            parts = [
                jnp.where(mine, wide(part.astype(F32), owners), 0.0)
                for part in two_parts(sums_ref[128 + h : 129 + h, :])
            ]
            pltpu.matmul_push_rhs(lanes, staging_register=1 - h, mxu_index=h, transpose=True)
            pltpu.matmul_acc_lhs(accs[2 + h], jnp.concatenate(parts, 0).astype(BF16), load_staged_rhs=1 - h)
        total = pltpu.matmul_pop(accs[0]) + pltpu.matmul_pop(accs[1])
        counts = pltpu.matmul_pop(accs[2]) + pltpu.matmul_pop(accs[3])
        tiles_ref[...] = (total[:, :128] + total[:, 128:]).reshape(owners, 8, 128)
        counts_ref[:, 0, :] = counts[:owners, :128] + counts[owners:, :128]

    pl.run_scoped(pick_slots, *[pltpu.ACC(q)((rows, 256), F32) for rows in (owners * 8, owners * 2) for q in range(2)])

    pairs = ((places_ref, got_places), (tiles_ref, got_tiles), (counts_ref, got_counts))

    @pl.loop(1, owners)
    def _(k):
        for n in (1, 2):
            send(n, *pairs[n], k)

    for source, landing in pairs:
        landing[me] = source[me]
    for n, (source, landing) in enumerate(pairs):
        whole = pltpu.make_async_remote_copy(
            src_ref=source.at[pl.ds(0, owners - 1)], dst_ref=landing.at[pl.ds(0, owners - 1)],
            send_sem=send_sems.at[n], recv_sem=recv_sems.at[n],
            device_id=(g, lax.rem(me + 1, owners)), device_id_type=MESH,
        )
        whole.wait_recv()
        whole.wait_send()

    def place_slots(*accs):
        place = jnp.sum(got_places[:, 0, :].reshape(owners // 8, 8, 128), axis=1)
        count = jnp.sum(got_counts[:, 0, :].reshape(owners // 8, 8, 128), axis=1)
        number = lax.broadcasted_iota(I32, (RANGE, 256), 0).astype(F32) + 1.0
        lane = lax.broadcasted_iota(I32, (16, 8, 128), 2)
        row16 = lax.broadcasted_iota(I32, (16, 256), 0)
        for i in range(owners // 16):
            q = i % 2
            put = onehot(wide(beside(place, i), RANGE) == number)
            tiles = got_tiles[16 * i : 16 * i + 16]
            split = jnp.stack([jnp.where(lane < 64, tiles, 0.0), jnp.where(lane < 64, 0.0, tiles)], 1)
            right = jnp.concatenate(two_parts(split.reshape(256, 128)), 1)
            pltpu.matmul_push_rhs(right, staging_register=0, mxu_index=q)
            pltpu.matmul_acc_lhs(accs[q], put, load_staged_rhs=0)
            high, rest = (wide(p.astype(F32), 16) for p in two_parts(beside(count, i)))
            marks = jnp.where(row16 == 0, high, jnp.where(row16 == 1, rest, 0.0)).astype(BF16)
            pltpu.matmul_push_rhs(put, staging_register=1, mxu_index=q, transpose=True)
            pltpu.matmul_acc_lhs(accs[2 + q], marks, load_staged_rhs=1)
        sums = pltpu.matmul_pop(accs[0]) + pltpu.matmul_pop(accs[1])
        counted = pltpu.matmul_pop(accs[2]) + pltpu.matmul_pop(accs[3])
        both = (sums[:, :128] + sums[:, 128:]).T
        ours[0:64] = both[:64] + both[64:]
        ours[64:72] = wide(counted[0:1] + counted[1:2], 8)

    pl.run_scoped(place_slots, *[pltpu.ACC(q)((rows, 256), F32) for rows in (RANGE, 16) for q in range(2)])

    def y_copy(k):
        return pltpu.make_async_remote_copy(
            src_ref=ours, dst_ref=theirs.at[k - 1], send_sem=y_send.at[k - 1], recv_sem=y_recv.at[k - 1],
            device_id=(lax.rem(g + k, groups), me), device_id_type=MESH,
        )

    for k in range(1, groups):
        y_copy(k).start()
    total = ours[...]
    for k in range(1, groups):
        y_copy(k).wait_recv()
        total = total + theirs[k - 1]
    out_ref[...] = total[0:64] / jnp.maximum(total[64:65], 1.0)
    for k in range(1, groups):
        y_copy(k).wait_send()


def body(labels, present, values):
    owners, groups = lax.axis_size("dev"), lax.axis_size("grp")
    times, pixels = values.shape[1:]
    lines = pixels // 128
    return pl.pallas_call(
        functools.partial(fused_kernel, owners, groups),
        out_shape=jax.ShapeDtypeStruct((times, RANGE), F32),
        in_specs=[VMEM, ANY, ANY],
        out_specs=VMEM,
        scratch_shapes=[
            pltpu.VMEM((CHUNKS, times, pixels // CHUNKS), BF16),
            pltpu.VMEM((lines, 128), I32),
            pltpu.VMEM((lines, 128), F32),
            pltpu.VMEM((lines, 128), F32),
            pltpu.VMEM((4, 128), I32),
            pltpu.VMEM((144, 256), F32),
            pltpu.VMEM((owners, 8, 128), F32),
            pltpu.VMEM((owners, 1, 128), F32),
            pltpu.VMEM((owners, 1, 128), F32),
            pltpu.VMEM((owners, 8, 128), F32),
            pltpu.VMEM((owners, 1, 128), F32),
            pltpu.VMEM((owners, 1, 128), F32),
            pltpu.VMEM((72, RANGE), F32),
            pltpu.VMEM((groups - 1, 72, RANGE), F32),
            pltpu.SemaphoreType.DMA((CHUNKS,)),
            pltpu.SemaphoreType.DMA,
            pltpu.SemaphoreType.DMA((3,)),
            pltpu.SemaphoreType.DMA((3,)),
            pltpu.SemaphoreType.DMA((groups - 1,)),
            pltpu.SemaphoreType.DMA((groups - 1,)),
        ],
        compiler_params=pltpu.CompilerParams(
            collective_id=0, has_side_effects=True, vmem_limit_bytes=VMEM_ALL
        ),
    )(present.reshape(4, 128), labels.reshape(lines, 128), values[0])


def solution(mesh):
    return jax.shard_map(
        body,
        mesh=mesh,
        in_specs=(P(("grp", "dev"), None), P(("grp", "dev"), None), P(("grp", "dev"), None, None)),
        out_specs=P(None, "dev"),
        check_vma=False,
    )
```

time: 119 us -> 37.6 us (0.32)
  Pallas kernels: 0 us -> 36 us
  matrix products: 35.3 us -> 0 us
  blocking collectives: 35.2 us -> 0 us
  local copies, waits for them, and re-layouts: 25 us -> 1.47 us
  other arithmetic: 21.8 us -> 0 us
    pallas_call x0 -> x1, Pallas kernels: none -> 36 us  [body(): pl.pallas_call(functools.partial(fused_kernel, owners, groups), out_shape...]
    dot_general x10 -> x0, matrix products: 35.3 us -> none  [the longest x8 34.1 us: accumulate(): lax.dot_general(block_values, one_hot, (((1,), (1,)), ((), ())), preferre...]
    all_to_all x2 -> x0, blocking collectives: 35.2 us -> none  [the longest x1 25.4 us: sent_together(): lax.all_to_all(both, axis, split_axis=split_dim, concat_axis=concat_dim,...]
    reduce_sum x10 -> x0, other arithmetic: 20.2 us -> none  [the longest x8 19.8 us: accumulate(): jnp.sum(one_hot, axis=1, dtype=jnp.float32)]
    gather x8 -> x0, local copies, waits for them, and re-layouts: 17.2 us -> none  [the longest x3 7.03 us: body(): jnp.take(local_place, source_slot).reshape(owner_count, capacity)]
    dynamic_slice x8 -> x0, local copies, waits for them, and re-layouts: 6.12 us -> none  [accumulate(): lax.dynamic_slice_in_dim(label_row, block_index * block_size, block_size)]
    unnamed x1, local copies, waits for them, and re-layouts: 0.04 us -> 1.47 us
where the time goes in v2:
time: 37.6 us; the launch traced here: 37.4 us
  Pallas kernels  36 us (96%)
  local copies, waits for them, and re-layouts  1.47 us (4%)
    pallas_call x1, Pallas kernels, body(): pl.pallas_call(functools.partial(fused_kernel, owners, groups), out_shape...  36 us
    unnamed x1, local copies, waits for them, and re-layouts  1.47 us

profile of v2, /device:TPU:1, one launch (start us, length us, event | category | flops | bytes accessed | tf_op | source)
XLA Modules:
  0.0 37.4 jit_solution(10306379107767346239)
XLA Ops:
  0.0 36.0 %shard_map.37 = f32[64,256]{1,0:T(8,128)} custom-call(s32[4,128]{1,0:T(4,128)} %bitcast.5, s32[512,128]{1,0:T(8,128)} %bitcast.4, bf16[64,65536]{1,0:T(8,128)(2,1)} %bitcast.3), custom_call_target="tpu_custom_call" | custom-call | tf_op jit(solution)/shard_map/pallas_call | solution.py:288
  36.0 1.5 %copy.5 = f32[64,256]{1,0:T(8,128)} copy(f32[64,256]{1,0:T(8,128)} %shard_map.37) | data formatting | bytes 131072

commit v3 on v2

--- a/solution.py
+++ b/solution.py
@@ -15,7 +15,7 @@
 MESH = pl.DeviceIdType.MESH
 VMEM = pl.BlockSpec(memory_space=pltpu.VMEM)
 ANY = pl.BlockSpec(memory_space=pl.ANY)
-VMEM_ALL = 67043328
+VMEM_LIMIT = 48 * 1024 * 1024
 
 
 def onehot(mask, dtype=BF16):
@@ -75,10 +75,10 @@
 
 
 def fused_kernel(
-    owners, groups, present_ref, labels_ref, values_ref, out_ref,
-    buf, lab_ref, lo_ref, hi_ref, slot_ref, sums_ref, tiles_ref, places_ref, counts_ref,
-    got_tiles, got_places, got_counts, ours, theirs,
-    in_sems, lab_sem, send_sems, recv_sems, y_send, y_recv,
+    owners, listed_ref, labels_ref, values_ref, out_ref,
+    buf, present_ref, lab_ref, lo_ref, hi_ref, table_ref, slot_ref, sums_ref, tiles_ref, places_ref, counts_ref,
+    got_tiles, got_places, got_counts, put_ref, ours, partial, theirs,
+    in_sems, listed_sem, lab_sem, send_sems, recv_sems, y_send, y_recv,
 ):
     g, me = lax.axis_index("grp"), lax.axis_index("dev")
     width = buf.shape[2]
@@ -90,31 +90,33 @@
             values_ref.at[:, pl.ds(pl.multiple_of(k * width, width), width)], buf.at[k], in_sems.at[k]
         )
 
+    listed_copy = pltpu.make_async_copy(listed_ref, present_ref, listed_sem)
+    listed_copy.start()
     lab_copy = pltpu.make_async_copy(labels_ref, lab_ref, lab_sem)
     lab_copy.start()
-    for k in range(CHUNKS):
-        chunk_copy(k).start()
-
     barrier = pltpu.get_barrier_semaphore()
 
-    @pl.loop(1, owners)
-    def _(k):
+    beside_g = (g + 1 - 2 * lax.rem(g, 2), 3 - g)
+    for k in range(1, owners):
+        if k == 8:
+            for n in range(CHUNKS):
+                chunk_copy(n).start()
         pl.semaphore_signal(barrier, inc=1, device_id=(g, lax.rem(me + k, owners)), device_id_type=MESH)
-
-    @pl.loop(1, groups)
-    def _(k):
-        pl.semaphore_signal(barrier, inc=1, device_id=(lax.rem(g + k, groups), me), device_id_type=MESH)
-
+    for other in beside_g:
+        pl.semaphore_signal(barrier, inc=1, device_id=(other, me), device_id_type=MESH)
+
+    listed_copy.wait()
     present = present_ref[...]
     owner_row = lax.broadcasted_iota(I32, (owners, 256), 0)
     lane_row = lax.broadcasted_iota(I32, (256, 256), 0)
     shift = (me & 7) * CAP
 
-    def clear(*accs):
-        for a in accs:
-            pltpu.matmul_pop(a)
-
-    pl.run_scoped(clear, *[pltpu.ACC(q)((1024, 256), F32) for q in range(2)])
+    def rank_chunk(k):
+        rows = pl.ds(pl.multiple_of(k * 64, 64), 64)
+        labels = lab_ref[rows, :]
+        ranked = [rank_of(labels[8 * i : 8 * i + 8], table_ref[...]) for i in range(8)]
+        lo_ref[rows, :] = jnp.concatenate([a for a, _ in ranked], 0).astype(F32)
+        hi_ref[rows, :] = jnp.concatenate([b for _, b in ranked], 0).astype(F32)
 
     def prepare(*accs):
         table = make_table(present, accs[:2])
@@ -129,21 +131,10 @@
             pltpu.matmul_push_rhs(lanes, staging_register=0, mxu_index=h, transpose=True)
             pltpu.matmul_acc_lhs(accs[2 + h], jnp.where(mine, number, 0.0).astype(BF16), load_staged_rhs=0)
         places_ref[:, 0, :] = (pltpu.matmul_pop(accs[2]) + pltpu.matmul_pop(accs[3]))[:, :128]
+        slot_ref[...] = slot
+        table_ref[...] = table
         lab_copy.wait()
-
-        @pl.loop(0, lo_ref.shape[0] // 64)
-        def _(i):
-            rows = pl.ds(pl.multiple_of(i * 64, 64), 64)
-            labels = lab_ref[rows, :]
-            low, high = [], []
-            for k in range(8):
-                a, b = rank_of(labels[8 * k : 8 * k + 8], table)
-                low.append(a)
-                high.append(b)
-            lo_ref[rows, :] = jnp.concatenate(low, 0).astype(F32)
-            hi_ref[rows, :] = jnp.concatenate(high, 0).astype(F32)
-
-        slot_ref[...] = slot
+        rank_chunk(0)
 
     pl.run_scoped(prepare, *[pltpu.ACC(q)((rows, 256), F32) for rows in (16, owners) for q in range(2)])
 
@@ -159,8 +150,9 @@
         row256 = lax.broadcasted_iota(I32, (256, 128), 0).astype(F32).astype(BF16)
         row16 = lax.broadcasted_iota(I32, (16, 128), 0).astype(F32).astype(BF16)
 
-        def chunk(k):
+        def chunk(k, beside_it=lambda: None):
             chunk_copy(k).wait()
+            beside_it()
             for j in range(steps):
                 q, reg = j % 2, (j // 2) % 2
                 hots, first, second, marks = [], [], [], []
@@ -180,10 +172,18 @@
                 pltpu.matmul_acc_lhs(accs[q][1], joined[2])
                 pltpu.matmul_acc_lhs(accs[q][2], joined[3])
 
-        pl.loop(0, CHUNKS - 2)(chunk)
-        pl.semaphore_wait(barrier, owners + groups - 2)
-        pl.loop(1, owners)(functools.partial(send, 0, places_ref, got_places))
-        pl.loop(CHUNKS - 2, CHUNKS)(chunk)
+        @pl.loop(0, CHUNKS - 1)
+        def _(k):
+            chunk(k)
+            rank_chunk(k + 1)
+
+        pl.semaphore_wait(barrier, owners + 1)
+
+        def send_places():
+            for k in range(1, owners):
+                send(0, places_ref, got_places, k)
+
+        chunk(CHUNKS - 1, send_places)
         for a, b, at, rows in zip(accs[0], accs[1], (0, 64, 128), (64, 64, 16)):
             sums_ref[at : at + rows, :] = pltpu.matmul_pop(a) + pltpu.matmul_pop(b)
 
@@ -222,14 +222,17 @@
 
     pairs = ((places_ref, got_places), (tiles_ref, got_tiles), (counts_ref, got_counts))
 
-    @pl.loop(1, owners)
-    def _(k):
-        for n in (1, 2):
-            send(n, *pairs[n], k)
+    @pl.loop(0, owners // 9)
+    def _(i):
+        for k in range(9):
+            for n in (1, 2):
+                send(n, *pairs[n], i * 9 + k + 1)
 
     for source, landing in pairs:
         landing[me] = source[me]
-    for n, (source, landing) in enumerate(pairs):
+
+    def arrived(n):
+        source, landing = pairs[n]
         whole = pltpu.make_async_remote_copy(
             src_ref=source.at[pl.ds(0, owners - 1)], dst_ref=landing.at[pl.ds(0, owners - 1)],
             send_sem=send_sems.at[n], recv_sem=recv_sems.at[n],
@@ -238,15 +241,21 @@
         whole.wait_recv()
         whole.wait_send()
 
+    arrived(0)
+    place = jnp.sum(got_places[:, 0, :].reshape(owners // 8, 8, 128), axis=1)
+    number = lax.broadcasted_iota(I32, (RANGE, 256), 0).astype(F32) + 1.0
+    for i in range(owners // 16):
+        put_ref[i] = onehot(wide(beside(place, i), RANGE) == number)
+    arrived(1)
+    arrived(2)
+
     def place_slots(*accs):
-        place = jnp.sum(got_places[:, 0, :].reshape(owners // 8, 8, 128), axis=1)
         count = jnp.sum(got_counts[:, 0, :].reshape(owners // 8, 8, 128), axis=1)
-        number = lax.broadcasted_iota(I32, (RANGE, 256), 0).astype(F32) + 1.0
         lane = lax.broadcasted_iota(I32, (16, 8, 128), 2)
         row16 = lax.broadcasted_iota(I32, (16, 256), 0)
         for i in range(owners // 16):
             q = i % 2
-            put = onehot(wide(beside(place, i), RANGE) == number)
+            put = put_ref[i]
             tiles = got_tiles[16 * i : 16 * i + 16]
             split = jnp.stack([jnp.where(lane < 64, tiles, 0.0), jnp.where(lane < 64, 0.0, tiles)], 1)
             right = jnp.concatenate(two_parts(split.reshape(256, 128)), 1)
@@ -264,37 +273,47 @@
 
     pl.run_scoped(place_slots, *[pltpu.ACC(q)((rows, 256), F32) for rows in (RANGE, 16) for q in range(2)])
 
-    def y_copy(k):
-        return pltpu.make_async_remote_copy(
-            src_ref=ours, dst_ref=theirs.at[k - 1], send_sem=y_send.at[k - 1], recv_sem=y_recv.at[k - 1],
-            device_id=(lax.rem(g + k, groups), me), device_id_type=MESH,
-        )
-
-    for k in range(1, groups):
-        y_copy(k).start()
+    halves = (pl.ds(0, 32), pl.ds(32, 40))
     total = ours[...]
-    for k in range(1, groups):
-        y_copy(k).wait_recv()
-        total = total + theirs[k - 1]
+    for step in range(2):
+        source = ours if step == 0 else partial
+        copies = []
+        for n, rows in enumerate(halves):
+            copies.append(
+                pltpu.make_async_remote_copy(
+                    src_ref=source.at[rows], dst_ref=theirs.at[step, rows], send_sem=y_send.at[2 * step + n],
+                    recv_sem=y_recv.at[2 * step + n], device_id=(beside_g[(step + n) % 2], me), device_id_type=MESH,
+                )
+            )
+        for copy in copies:
+            copy.start()
+        for copy in copies:
+            copy.wait_recv()
+        total = total + theirs[step]
+        if step == 0:
+            partial[...] = total
+        for copy in copies:
+            copy.wait_send()
     out_ref[...] = total[0:64] / jnp.maximum(total[64:65], 1.0)
-    for k in range(1, groups):
-        y_copy(k).wait_send()
 
 
 def body(labels, present, values):
     owners, groups = lax.axis_size("dev"), lax.axis_size("grp")
+    assert owners == 64 and groups == 4
     times, pixels = values.shape[1:]
     lines = pixels // 128
     return pl.pallas_call(
-        functools.partial(fused_kernel, owners, groups),
+        functools.partial(fused_kernel, owners),
         out_shape=jax.ShapeDtypeStruct((times, RANGE), F32),
-        in_specs=[VMEM, ANY, ANY],
+        in_specs=[ANY, ANY, ANY],
         out_specs=VMEM,
         scratch_shapes=[
             pltpu.VMEM((CHUNKS, times, pixels // CHUNKS), BF16),
+            pltpu.VMEM((4, 128), I32),
             pltpu.VMEM((lines, 128), I32),
             pltpu.VMEM((lines, 128), F32),
             pltpu.VMEM((lines, 128), F32),
+            pltpu.VMEM((8, 128), I32),
             pltpu.VMEM((4, 128), I32),
             pltpu.VMEM((144, 256), F32),
             pltpu.VMEM((owners, 8, 128), F32),
@@ -303,19 +322,26 @@
             pltpu.VMEM((owners, 8, 128), F32),
             pltpu.VMEM((owners, 1, 128), F32),
             pltpu.VMEM((owners, 1, 128), F32),
+            pltpu.VMEM((owners // 16, RANGE, 256), BF16),
             pltpu.VMEM((72, RANGE), F32),
-            pltpu.VMEM((groups - 1, 72, RANGE), F32),
+            pltpu.VMEM((72, RANGE), F32),
+            pltpu.VMEM((2, 72, RANGE), F32),
             pltpu.SemaphoreType.DMA((CHUNKS,)),
+            pltpu.SemaphoreType.DMA,
             pltpu.SemaphoreType.DMA,
             pltpu.SemaphoreType.DMA((3,)),
             pltpu.SemaphoreType.DMA((3,)),
-            pltpu.SemaphoreType.DMA((groups - 1,)),
-            pltpu.SemaphoreType.DMA((groups - 1,)),
+            pltpu.SemaphoreType.DMA((4,)),
+            pltpu.SemaphoreType.DMA((4,)),
         ],
         compiler_params=pltpu.CompilerParams(
-            collective_id=0, has_side_effects=True, vmem_limit_bytes=VMEM_ALL
+            collective_id=0, has_side_effects=True, vmem_limit_bytes=VMEM_LIMIT
         ),
-    )(present.reshape(4, 128), labels.reshape(lines, 128), values[0])
+    )(
+        pltpu.with_memory_space_constraint(present.reshape(4, 128), pltpu.HBM),
+        pltpu.with_memory_space_constraint(labels.reshape(lines, 128), pltpu.HBM),
+        pltpu.with_memory_space_constraint(values[0], pltpu.HBM),
+    )
 
 
 def solution(mesh):

time: 37.6 us -> 31.1 us (0.83)
  Pallas kernels: 36 us -> 30.1 us
  local copies, waits for them, and re-layouts: 1.47 us -> 0.63 us
    pallas_call x1, Pallas kernels: 36 us -> 30.1 us  [body(): pl.pallas_call(functools.partial(fused_kernel, owners), out_shape=jax.Sha...]
    unnamed x1, local copies, waits for them, and re-layouts: 1.47 us -> 0.63 us
where the time goes in v3:
time: 31.1 us; the launch traced here: 30.7 us
  Pallas kernels  30.1 us (97%)
  local copies, waits for them, and re-layouts  0.63 us (2%)
    pallas_call x1, Pallas kernels, body(): pl.pallas_call(functools.partial(fused_kernel, owners), out_shape=jax.Sha...  30.1 us
    unnamed x1, local copies, waits for them, and re-layouts  0.63 us

profile of v3, /device:TPU:1, one launch (start us, length us, event | category | flops | bytes accessed | tf_op | source)
XLA Modules:
  0.0 30.7 jit_solution(12962772589451324168)
XLA Ops:
  0.0 30.1 %shard_map.37 = f32[64,256]{1,0:T(8,128)S(1)} custom-call(s32[4,128]{1,0:T(4,128)} %bitcast.5, s32[512,128]{1,0:T(8,128)} %bitcast.4, bf16[64,65536]{1,0:T(8,128)(2,1)} %bitcast.3), custom_call_target="tpu_custom_call" | custom-call | tf_op jit(solution)/shard_map/pallas_call | solution.py:305
  30.1 0.6 %copy.5 = f32[64,256]{1,0:T(8,128)} copy(f32[64,256]{1,0:T(8,128)S(1)} %shard_map.37) | data formatting | bytes 131072

commit v4 on v3

--- a/solution.py
+++ b/solution.py
@@ -11,6 +11,7 @@
 RANGE = 256
 CAP = 16
 CHUNKS = 8
+PARTS = 4
 F32, BF16, F8, I32 = jnp.float32, jnp.bfloat16, jnp.float8_e4m3fn, jnp.int32
 MESH = pl.DeviceIdType.MESH
 VMEM = pl.BlockSpec(memory_space=pltpu.VMEM)
@@ -42,7 +43,7 @@
     below = (jnp.full_like(bit, 1) << bit) - 1
     rank = (entry >> 16) + lax.population_count(entry & 65535 & below)
     listed = ((entry >> bit) & 1) == 1
-    return rank & 255, jnp.where(listed, rank >> 8, 8)
+    return rank & 255, jnp.where(listed, rank >> 8, 7)
 
 
 def wide(row, rows):
@@ -76,8 +77,8 @@
 
 def fused_kernel(
     owners, listed_ref, labels_ref, values_ref, out_ref,
-    buf, present_ref, lab_ref, lo_ref, hi_ref, table_ref, slot_ref, sums_ref, tiles_ref, places_ref, counts_ref,
-    got_tiles, got_places, got_counts, put_ref, ours, partial, theirs,
+    buf, present_ref, lab_ref, lo_ref, hi_ref, table_ref, slot_ref, sums_ref, tiles_ref, rows_ref,
+    got_tiles, got_rows, put_ref, ours, partial, theirs,
     in_sems, listed_sem, lab_sem, send_sems, recv_sems, y_send, y_recv,
 ):
     g, me = lax.axis_index("grp"), lax.axis_index("dev")
@@ -108,8 +109,8 @@
     listed_copy.wait()
     present = present_ref[...]
     owner_row = lax.broadcasted_iota(I32, (owners, 256), 0)
-    lane_row = lax.broadcasted_iota(I32, (256, 256), 0)
-    shift = (me & 7) * CAP
+    lane_row = lax.broadcasted_iota(I32, (128, 256), 0)
+    shift = me // 16 * (2 * CAP)
 
     def rank_chunk(k):
         rows = pl.ds(pl.multiple_of(k * 64, 64), 64)
@@ -123,36 +124,30 @@
         first = lookup(table, (present >> 8) << 4) >> 16
         index = lax.broadcasted_iota(I32, present.shape, 0) * 128 + lax.broadcasted_iota(I32, present.shape, 1)
         slot = index - first
-        for h in range(2):
-            zone, at = beside(present, h), beside(slot, h)
-            mine = wide(zone >> 8, owners) == owner_row
-            lanes = onehot(wide(at, 256) + shift == lane_row)
-            number = wide(((zone & 255) + 1).astype(F32), owners)
-            pltpu.matmul_push_rhs(lanes, staging_register=0, mxu_index=h, transpose=True)
-            pltpu.matmul_acc_lhs(accs[2 + h], jnp.where(mine, number, 0.0).astype(BF16), load_staged_rhs=0)
-        places_ref[:, 0, :] = (pltpu.matmul_pop(accs[2]) + pltpu.matmul_pop(accs[3]))[:, :128]
         slot_ref[...] = slot
         table_ref[...] = table
         lab_copy.wait()
         rank_chunk(0)
 
-    pl.run_scoped(prepare, *[pltpu.ACC(q)((rows, 256), F32) for rows in (16, owners) for q in range(2)])
-
-    def send(n, source, landing, k):
+    pl.run_scoped(prepare, *[pltpu.ACC(q)((rows, 256), F32) for rows in (16,) for q in range(2)])
+
+    def send(n, k):
+        source, landing = pairs[n]
         to = lax.rem(me + k, owners)
         pltpu.make_async_remote_copy(
-            src_ref=source.at[to], dst_ref=landing.at[me], send_sem=send_sems.at[n],
+            src_ref=source.at[k], dst_ref=landing.at[me], send_sem=send_sems.at[n],
             recv_sem=recv_sems.at[n], device_id=(g, to), device_id_type=MESH,
         ).start()
+
+    pairs = ((rows_ref, got_rows), (tiles_ref, got_tiles))
 
     def add_up(*refs):
         accs = (refs[:3], refs[3:])
         row256 = lax.broadcasted_iota(I32, (256, 128), 0).astype(F32).astype(BF16)
-        row16 = lax.broadcasted_iota(I32, (16, 128), 0).astype(F32).astype(BF16)
-
-        def chunk(k, beside_it=lambda: None):
+        row8 = lax.broadcasted_iota(I32, (8, 128), 0).astype(F32)
+
+        def chunk(k):
             chunk_copy(k).wait()
-            beside_it()
             for j in range(steps):
                 q, reg = j % 2, (j // 2) % 2
                 hots, first, second, marks = [], [], [], []
@@ -165,7 +160,7 @@
                     high64 = jnp.tile(high, (4, 1))
                     first.append(jnp.where(high64 == zero, pixels, zero))
                     second.append(jnp.where(high64 == one, pixels, zero))
-                    marks.append(jnp.where(high == row16, one, zero))
+                    marks.append(jnp.where(wide(hi_ref[pl.ds(row, 1), :], 8) == row8, 1.0, 0.0))
                 joined = [jnp.concatenate(p, 1) for p in (hots, first, second, marks)]
                 pltpu.matmul_push_rhs(joined[0], staging_register=reg, mxu_index=q, transpose=True)
                 pltpu.matmul_acc_lhs(accs[q][0], joined[1], load_staged_rhs=reg)
@@ -177,59 +172,63 @@
             chunk(k)
             rank_chunk(k + 1)
 
-        pl.semaphore_wait(barrier, owners + 1)
-
-        def send_places():
-            for k in range(1, owners):
-                send(0, places_ref, got_places, k)
-
-        chunk(CHUNKS - 1, send_places)
-        for a, b, at, rows in zip(accs[0], accs[1], (0, 64, 128), (64, 64, 16)):
+        chunk(CHUNKS - 1)
+        for a, b, at, rows in zip(accs[0], accs[1], (0, 64, 128), (64, 64, 8)):
             sums_ref[at : at + rows, :] = pltpu.matmul_pop(a) + pltpu.matmul_pop(b)
 
-    pl.run_scoped(add_up, *[pltpu.ACC(q)((rows, 256), F32) for q in range(2) for rows in (64, 64, 16)])
+    pl.run_scoped(add_up, *[pltpu.ACC(q)((rows, 256), F32) for q in range(2) for rows in (64, 64, 8)])
+
+    pl.semaphore_wait(barrier, owners + 1)
 
     def pick_slots(*accs):
         slot = slot_ref[...]
-        pair_row = lax.broadcasted_iota(I32, (owners * 8, 256), 0)
+        part_rows = owners * 8 // PARTS
+        pair_row = lax.broadcasted_iota(I32, (part_rows, 256), 0)
         empty = jnp.zeros((64, 256), BF16)
         for h in range(2):
             zone, at = beside(present, h), beside(slot, h)
-            owner = zone >> 8
+            mine = wide(((zone >> 8) + (owners - me)) & (owners - 1), owners) == owner_row
+            lanes = wide(at, 128) + shift
+            lanes = jnp.concatenate([onehot(lanes == lane_row), onehot(lanes + CAP == lane_row)], 0)
+            parts = [((zone & 255) + 1).astype(F32)]
+            parts += [part.astype(F32) for part in two_parts(sums_ref[128 + h : 129 + h, :])]
+            left = jnp.concatenate([jnp.where(mine, wide(part, owners), 0.0) for part in parts], 0)
+            pltpu.matmul_push_rhs(lanes, staging_register=0, mxu_index=h, transpose=True)
+            pltpu.matmul_acc_lhs(accs[h], left.astype(BF16), load_staged_rhs=0)
+        found = pltpu.matmul_pop(accs[0]) + pltpu.matmul_pop(accs[1])
+        rows_ref[:, 0, :] = (
+            found[:owners, :128] + found[owners : 2 * owners, 128:] + found[2 * owners :, 128:]
+        )
+        for k in range(1, owners):
+            send(0, k)
+        for h in range(2):
+            zone, at = beside(present, h), beside(slot, h)
+            owner = ((zone >> 8) + (owners - me)) & (owners - 1)
             target = ((owner << 3) + (at & 7)) * 2 + (at >> 3)
             high, rest = two_parts(sums_ref[64 * h : 64 * h + 64, :])
             for parity in range(2):
-                order = (high, empty, rest, empty) if parity == 0 else (empty, high, empty, rest)
+                parts = (high, empty, rest, empty) if parity == 0 else (empty, high, empty, rest)
                 pltpu.matmul_push_rhs(
-                    jnp.concatenate(order, 0), staging_register=h, mxu_index=parity, transpose=True
+                    jnp.concatenate(parts, 0), staging_register=h, mxu_index=parity, transpose=True
                 )
-                pick = onehot(wide(target, owners * 8) == pair_row * 2 + parity)
-                pltpu.matmul_acc_lhs(accs[parity], pick, load_staged_rhs=h)
-            mine = wide(owner, owners) == owner_row
-            lanes = onehot(wide(at, 256) + shift == lane_row)
-            parts = [
-                jnp.where(mine, wide(part.astype(F32), owners), 0.0)
-                for part in two_parts(sums_ref[128 + h : 129 + h, :])
-            ]
-            pltpu.matmul_push_rhs(lanes, staging_register=1 - h, mxu_index=h, transpose=True)
-            pltpu.matmul_acc_lhs(accs[2 + h], jnp.concatenate(parts, 0).astype(BF16), load_staged_rhs=1 - h)
-        total = pltpu.matmul_pop(accs[0]) + pltpu.matmul_pop(accs[1])
-        counts = pltpu.matmul_pop(accs[2]) + pltpu.matmul_pop(accs[3])
-        tiles_ref[...] = (total[:, :128] + total[:, 128:]).reshape(owners, 8, 128)
-        counts_ref[:, 0, :] = counts[:owners, :128] + counts[owners:, :128]
-
-    pl.run_scoped(pick_slots, *[pltpu.ACC(q)((rows, 256), F32) for rows in (owners * 8, owners * 2) for q in range(2)])
-
-    pairs = ((places_ref, got_places), (tiles_ref, got_tiles), (counts_ref, got_counts))
-
-    @pl.loop(0, owners // 9)
-    def _(i):
-        for k in range(9):
-            for n in (1, 2):
-                send(n, *pairs[n], i * 9 + k + 1)
+            for part in range(PARTS):
+                for parity in range(2):
+                    pick = onehot(wide(target, part_rows) == (pair_row + part * part_rows) * 2 + parity)
+                    pltpu.matmul_acc_lhs(
+                        accs[2 + 2 * part + parity], pick, load_staged_rhs=h if part == 0 else None
+                    )
+        for part in range(PARTS):
+            total = pltpu.matmul_pop(accs[2 + 2 * part]) + pltpu.matmul_pop(accs[3 + 2 * part])
+            first = part * owners // PARTS
+            tiles_ref[first : first + owners // PARTS] = (total[:, :128] + total[:, 128:]).reshape(-1, 8, 128)
+            for k in range(max(first, 1), first + owners // PARTS):
+                send(1, k)
+
+    shapes = (owners * 3,) + (owners * 8 // PARTS,) * PARTS
+    pl.run_scoped(pick_slots, *[pltpu.ACC(q)((rows, 256), F32) for rows in shapes for q in range(2)])
 
     for source, landing in pairs:
-        landing[me] = source[me]
+        landing[me] = source[0]
 
     def arrived(n):
         source, landing = pairs[n]
@@ -242,21 +241,25 @@
         whole.wait_send()
 
     arrived(0)
-    place = jnp.sum(got_places[:, 0, :].reshape(owners // 8, 8, 128), axis=1)
+    rows = got_rows[:, 0, :]
+    joined = rows[0:16] + rows[16:32] + rows[32:48] + rows[48:64]
+    even = (lax.broadcasted_iota(I32, (8, 128), 1) & CAP) == 0
+    place = jnp.where(even, joined[:8], pltpu.roll(joined[8:], CAP, 1))
+    count = jnp.where(even, pltpu.roll(joined[:8], 128 - CAP, 1), joined[8:])
     number = lax.broadcasted_iota(I32, (RANGE, 256), 0).astype(F32) + 1.0
     for i in range(owners // 16):
         put_ref[i] = onehot(wide(beside(place, i), RANGE) == number)
     arrived(1)
-    arrived(2)
 
     def place_slots(*accs):
-        count = jnp.sum(got_counts[:, 0, :].reshape(owners // 8, 8, 128), axis=1)
         lane = lax.broadcasted_iota(I32, (16, 8, 128), 2)
         row16 = lax.broadcasted_iota(I32, (16, 256), 0)
         for i in range(owners // 16):
             q = i % 2
             put = put_ref[i]
-            tiles = got_tiles[16 * i : 16 * i + 16]
+            tiles = jnp.stack(
+                [got_tiles[16 * a + 8 * b + r] for r in (2 * i, 2 * i + 1) for a in range(4) for b in range(2)], 0
+            )
             split = jnp.stack([jnp.where(lane < 64, tiles, 0.0), jnp.where(lane < 64, 0.0, tiles)], 1)
             right = jnp.concatenate(two_parts(split.reshape(256, 128)), 1)
             pltpu.matmul_push_rhs(right, staging_register=0, mxu_index=q)
@@ -315,12 +318,10 @@
             pltpu.VMEM((lines, 128), F32),
             pltpu.VMEM((8, 128), I32),
             pltpu.VMEM((4, 128), I32),
-            pltpu.VMEM((144, 256), F32),
+            pltpu.VMEM((136, 256), F32),
             pltpu.VMEM((owners, 8, 128), F32),
             pltpu.VMEM((owners, 1, 128), F32),
-            pltpu.VMEM((owners, 1, 128), F32),
             pltpu.VMEM((owners, 8, 128), F32),
-            pltpu.VMEM((owners, 1, 128), F32),
             pltpu.VMEM((owners, 1, 128), F32),
             pltpu.VMEM((owners // 16, RANGE, 256), BF16),
             pltpu.VMEM((72, RANGE), F32),
@@ -329,8 +330,8 @@
             pltpu.SemaphoreType.DMA((CHUNKS,)),
             pltpu.SemaphoreType.DMA,
             pltpu.SemaphoreType.DMA,
-            pltpu.SemaphoreType.DMA((3,)),
-            pltpu.SemaphoreType.DMA((3,)),
+            pltpu.SemaphoreType.DMA((2,)),
+            pltpu.SemaphoreType.DMA((2,)),
             pltpu.SemaphoreType.DMA((4,)),
             pltpu.SemaphoreType.DMA((4,)),
         ],

time: 31.1 us -> 30.5 us (0.981)
  Pallas kernels: 30.1 us -> 29.3 us
    pallas_call x1, Pallas kernels: 30.1 us -> 29.3 us  [body(): pl.pallas_call(functools.partial(fused_kernel, owners), out_shape=jax.Sha...]
where the time goes in v4:
time: 30.5 us; the launch traced here: 30 us
  Pallas kernels  29.3 us (96%)
  local copies, waits for them, and re-layouts  0.63 us (2%)
    pallas_call x1, Pallas kernels, body(): pl.pallas_call(functools.partial(fused_kernel, owners), out_shape=jax.Sha...  29.3 us
    unnamed x1, local copies, waits for them, and re-layouts  0.63 us

profile of v4, /device:TPU:1, one launch (start us, length us, event | category | flops | bytes accessed | tf_op | source)
XLA Modules:
  0.0 30.0 jit_solution(14323738180239897627)
XLA Ops:
  0.0 29.3 %shard_map.37 = f32[64,256]{1,0:T(8,128)S(1)} custom-call(s32[4,128]{1,0:T(4,128)} %bitcast.5, s32[512,128]{1,0:T(8,128)} %bitcast.4, bf16[64,65536]{1,0:T(8,128)(2,1)} %bitcast.3), custom_call_target="tpu_custom_call" | custom-call | tf_op jit(solution)/shard_map/pallas_call | solution.py:308
  29.3 0.6 %copy.5 = f32[64,256]{1,0:T(8,128)} copy(f32[64,256]{1,0:T(8,128)S(1)} %shard_map.37) | data formatting | bytes 131072

commit v5 on v4

--- a/solution.py
+++ b/solution.py
@@ -276,28 +276,34 @@
 
     pl.run_scoped(place_slots, *[pltpu.ACC(q)((rows, 256), F32) for rows in (RANGE, 16) for q in range(2)])
 
-    halves = (pl.ds(0, 32), pl.ds(32, 40))
-    total = ours[...]
+    pieces = ((48, 24, 1), (0, 16, 0), (32, 16, 1), (16, 16, 0))
+
+    def y_copy(step, n):
+        at, rows, turn = pieces[n]
+        source = ours if step == 0 else partial
+        return pltpu.make_async_remote_copy(
+            src_ref=source.at[pl.ds(at, rows)], dst_ref=theirs.at[step, pl.ds(at, rows)],
+            send_sem=y_send.at[4 * step + n], recv_sem=y_recv.at[4 * step + n],
+            device_id=(beside_g[(step + turn) % 2], me), device_id_type=MESH,
+        )
+
+    for n in range(4):
+        y_copy(0, n).start()
+    for n, (at, rows, _) in enumerate(pieces):
+        y_copy(0, n).wait_recv()
+        partial[at : at + rows] = ours[at : at + rows] + theirs[0, at : at + rows]
+        y_copy(1, n).start()
+    counts = None
+    for n, (at, rows, _) in enumerate(pieces):
+        y_copy(1, n).wait_recv()
+        total = partial[at : at + rows] + theirs[1, at : at + rows]
+        if n == 0:
+            counts = jnp.maximum(total[16:17], 1.0)
+            total = total[:16]
+        out_ref[at : at + 16] = total / counts
     for step in range(2):
-        source = ours if step == 0 else partial
-        copies = []
-        for n, rows in enumerate(halves):
-            copies.append(
-                pltpu.make_async_remote_copy(
-                    src_ref=source.at[rows], dst_ref=theirs.at[step, rows], send_sem=y_send.at[2 * step + n],
-                    recv_sem=y_recv.at[2 * step + n], device_id=(beside_g[(step + n) % 2], me), device_id_type=MESH,
-                )
-            )
-        for copy in copies:
-            copy.start()
-        for copy in copies:
-            copy.wait_recv()
-        total = total + theirs[step]
-        if step == 0:
-            partial[...] = total
-        for copy in copies:
-            copy.wait_send()
-    out_ref[...] = total[0:64] / jnp.maximum(total[64:65], 1.0)
+        for n in range(4):
+            y_copy(step, n).wait_send()
 
 
 def body(labels, present, values):
@@ -332,8 +338,8 @@
             pltpu.SemaphoreType.DMA,
             pltpu.SemaphoreType.DMA((2,)),
             pltpu.SemaphoreType.DMA((2,)),
-            pltpu.SemaphoreType.DMA((4,)),
-            pltpu.SemaphoreType.DMA((4,)),
+            pltpu.SemaphoreType.DMA((8,)),
+            pltpu.SemaphoreType.DMA((8,)),
         ],
         compiler_params=pltpu.CompilerParams(
             collective_id=0, has_side_effects=True, vmem_limit_bytes=VMEM_LIMIT

time: 30.5 us -> 30.4 us (level)
  no operation moved by 1% of the time
where the time goes in v5:
time: 30.4 us; the launch traced here: 29.9 us
  Pallas kernels  29.2 us (96%)
  local copies, waits for them, and re-layouts  0.63 us (2%)
    pallas_call x1, Pallas kernels, body(): pl.pallas_call(functools.partial(fused_kernel, owners), out_shape=jax.Sha...  29.2 us
    unnamed x1, local copies, waits for them, and re-layouts  0.63 us

profile of v5, /device:TPU:1, one launch (start us, length us, event | category | flops | bytes accessed | tf_op | source)
XLA Modules:
  0.0 29.9 jit_solution(15453510289426962884)
XLA Ops:
  0.0 29.2 %shard_map.37 = f32[64,256]{1,0:T(8,128)S(1)} custom-call(s32[4,128]{1,0:T(4,128)} %bitcast.5, s32[512,128]{1,0:T(8,128)} %bitcast.4, bf16[64,65536]{1,0:T(8,128)(2,1)} %bitcast.3), custom_call_target="tpu_custom_call" | custom-call | tf_op jit(solution)/shard_map/pallas_call | solution.py:314
  29.2 0.6 %copy.5 = f32[64,256]{1,0:T(8,128)} copy(f32[64,256]{1,0:T(8,128)S(1)} %shard_map.37) | data formatting | bytes 131072

commit v6 on v5

--- a/solution.py
+++ b/solution.py
@@ -230,17 +230,15 @@
     for source, landing in pairs:
         landing[me] = source[0]
 
-    def arrived(n):
+    def whole(n):
         source, landing = pairs[n]
-        whole = pltpu.make_async_remote_copy(
+        return pltpu.make_async_remote_copy(
             src_ref=source.at[pl.ds(0, owners - 1)], dst_ref=landing.at[pl.ds(0, owners - 1)],
             send_sem=send_sems.at[n], recv_sem=recv_sems.at[n],
             device_id=(g, lax.rem(me + 1, owners)), device_id_type=MESH,
         )
-        whole.wait_recv()
-        whole.wait_send()
-
-    arrived(0)
+
+    whole(0).wait_recv()
     rows = got_rows[:, 0, :]
     joined = rows[0:16] + rows[16:32] + rows[32:48] + rows[48:64]
     even = (lax.broadcasted_iota(I32, (8, 128), 1) & CAP) == 0
@@ -249,7 +247,7 @@
     number = lax.broadcasted_iota(I32, (RANGE, 256), 0).astype(F32) + 1.0
     for i in range(owners // 16):
         put_ref[i] = onehot(wide(beside(place, i), RANGE) == number)
-    arrived(1)
+    whole(1).wait_recv()
 
     def place_slots(*accs):
         lane = lax.broadcasted_iota(I32, (16, 8, 128), 2)
@@ -301,6 +299,8 @@
             counts = jnp.maximum(total[16:17], 1.0)
             total = total[:16]
         out_ref[at : at + 16] = total / counts
+    for n in range(2):
+        whole(n).wait_send()
     for step in range(2):
         for n in range(4):
             y_copy(step, n).wait_send()

time: 30.4 us -> 30.4 us (level)
  no operation moved by 1% of the time
where the time goes in v6:
time: 30.4 us; the launch traced here: 29.9 us
  Pallas kernels  29.2 us (96%)
  local copies, waits for them, and re-layouts  0.63 us (2%)
    pallas_call x1, Pallas kernels, body(): pl.pallas_call(functools.partial(fused_kernel, owners), out_shape=jax.Sha...  29.2 us
    unnamed x1, local copies, waits for them, and re-layouts  0.63 us

profile of v6, /device:TPU:1, one launch (start us, length us, event | category | flops | bytes accessed | tf_op | source)
XLA Modules:
  0.0 29.9 jit_solution(7408233801295258779)
XLA Ops:
  0.0 29.2 %shard_map.37 = f32[64,256]{1,0:T(8,128)S(1)} custom-call(s32[4,128]{1,0:T(4,128)} %bitcast.5, s32[512,128]{1,0:T(8,128)} %bitcast.4, bf16[64,65536]{1,0:T(8,128)(2,1)} %bitcast.3), custom_call_target="tpu_custom_call" | custom-call | tf_op jit(solution)/shard_map/pallas_call | solution.py:314
  29.2 0.6 %copy.5 = f32[64,256]{1,0:T(8,128)} copy(f32[64,256]{1,0:T(8,128)S(1)} %shard_map.37) | data formatting | bytes 131072
